TPU v7x, 32 devices: a whole 2x2x4 slice. The times are simulated.
32 devices in a mesh: space: 8 (over z, x), tm: 4 (over y, core).
Axes of the slice: x: 2, y: 2, z: 4, core: 2. Of those that a mesh axis runs over, the one named last changes fastest.
Arguments:
- snapshots: float32 [16384, 4096], P('space', 'tm'), may hold values from -3000 to 3000, as said below
- sketch: float32 [4096, 256], P('tm'), may hold values from -6 to 6
Outputs:
- refined: float32 [16384, 256], P('space')
- cosample: float32 [4096, 256], P('tm')
Inputs may be any that keep to these rules, and one draw needn't show every extreme that they name: `snapshots`: float32 snapshot values.
All inputs are finite; a program needn't handle non-finite values.
Results may differ from a plain program's by a relative error of at most 0.000071.
Values sent between devices are 32-bit elements; how exact they have to be, the bound alone decides.
No kernel may reach another device: no remote copies, remote signals or barrier semaphores. Data moves between devices by JAX's collectives and lax.ppermute only.
A program may use at most 64 MiB of HBM per device.

v0:
```python
import jax
import jax.numpy as jnp
from jax import lax
from jax.sharding import PartitionSpec as P

EPS = 1e-06


def scale_rows(value):
    return value * lax.rsqrt(jnp.mean(value * value, axis=1, keepdims=True) + EPS)


def forward(block, right):
    return jnp.dot(
        block, right, precision=lax.Precision.HIGHEST, preferred_element_type=jnp.float32
    )


def backward(block, right):
    return lax.dot_general(
        block,
        right,
        (((0,), (0,)), ((), ())),
        precision=lax.Precision.HIGHEST,
        preferred_element_type=jnp.float32,
    )


def local(snapshots, sketch):
    sample = scale_rows(lax.psum(forward(snapshots, sketch), "tm"))
    cosample = scale_rows(lax.psum(backward(snapshots, sample), "space"))
    refined = scale_rows(lax.psum(forward(snapshots, cosample), "tm"))
    return (refined, cosample)


def solution(mesh):
    return jax.shard_map(
        local,
        mesh=mesh,
        in_specs=(P("space", "tm"), P("tm", None)),
        out_specs=(P("space", None), P("tm", None)),
        check_vma=False,
    )
```

profile of v0, /device:TPU:0, one launch (start us, length us, event | category | flops | bytes accessed | tf_op | source)
XLA Modules:
  0.0 239.9 jit_solution(7277704082778066408)
XLA Ops:
  7.2 0.0 copy-start
  7.2 0.0 all-reduce.4.cloned.1.call-start
  7.2 1.2 copy-done
  8.4 10.0 %fusion.6 = f32[2048,256]{1,0:T(8,128)} fusion(f32[2048,1024]{1,0:T(8,128)} %param.2, f32[1024,256]{1,0:T(8,128)S(1)} %copy-done), kind=kOutput, calls=%fused_computation.13 | convolution fusion | flops 6442450944 | bytes 11534336 | tf_op jit(solution)/shard_map/dot_general | solution.py:14
  18.4 0.0 all-reduce.4.cloned.1.call-update
  18.4 0.0 all-reduce.6.cloned.1.call-start
  18.5 54.2 %all-reduce.4.cloned.1.call-done = f32[2048,256]{1,0:T(8,128)} async-done(((f32[2048,256]{1,0:T(8,128)}), f32[2048,256]{1,0:T(8,128)}) %all-reduce.4.cloned.1.call-update) | async-done | bytes 2097168 | tf_op jit(solution)/shard_map/psum | solution.py:30
  72.7 0.0 copy-start.2
  72.7 2.1 multiply_reduce_fusion.1
  74.8 0.1 copy-done.2
  74.9 11.2 %fusion.2 = f32[1024,256]{0,1:T(8,128)} fusion(f32[2048,1024]{1,0:T(8,128)} %param.2, f32[2048,256]{1,0:T(8,128)S(1)} %copy-done.2, f32[2048]{0:T(1024)S(1)} %add_rsqrt_fusion.1), kind=kOutput, calls=%fused_computation.5 | convolution fusion | flops 6442975232 | bytes 11542528 | tf_op jit(solution)/shard_map/dot_general | solution.py:20
  86.1 0.0 all-reduce.6.cloned.1.call-update
  86.1 0.2 all-reduce.8.cloned.1.call-start
  86.3 78.2 %all-reduce.6.cloned.1.call-done = f32[1024,256]{0,1:T(8,128)} async-done(((f32[1024,256]{0,1:T(8,128)}), f32[1024,256]{0,1:T(8,128)}) %all-reduce.6.cloned.1.call-update) | async-done | bytes 1048592 | tf_op jit(solution)/shard_map/psum | solution.py:31
  164.6 1.3 multiply_reduce_fusion.2
  165.9 1.3 broadcast_multiply_fusion.1
  167.2 10.6 %convolution_bitcast_fusion = f32[2048,256]{0,1:T(8,128)} fusion(f32[1024,256]{0,1:T(8,128)S(1)} %broadcast_multiply_fusion.1, f32[2048,1024]{1,0:T(8,128)} %param.2), kind=kOutput, calls=%fused_computation | convolution fusion | flops 6442450944 | bytes 11534336 | tf_op jit(solution)/shard_map/dot_general | solution.py:14
  177.8 0.0 all-reduce.8.cloned.1.call-update
  177.8 1.3 copy.5
  179.2 49.8 %all-reduce.8.cloned.1.call-done = f32[2048,256]{0,1:T(8,128)} async-done(((f32[2048,256]{0,1:T(8,128)}), f32[2048,256]{0,1:T(8,128)}) %all-reduce.8.cloned.1.call-update) | async-done | bytes 2097168 | tf_op jit(solution)/shard_map/psum | solution.py:32
  229.0 1.9 multiply_reduce_fusion
  230.9 0.3 copy-done.1
  231.2 0.3 broadcast_multiply_fusion
  231.5 1.8 copy.4
  (4 shorter events, 0.0 us)
Async XLA Ops:
  7.2 1.2 copy-start
  7.2 65.5 %all-reduce.4.cloned.1.call-start = ((), (), s32[]{:S(2)}) async-start(), calls=%async_computation | async-start | bytes 4194304 | tf_op jit(solution)/shard_map/psum | solution.py:30
  18.4 146.1 %all-reduce.6.cloned.1.call-start = ((), (), s32[]{:S(2)}) async-start(), calls=%async_computation.1 | async-start | bytes 2097152 | tf_op jit(solution)/shard_map/psum | solution.py:31
  72.7 2.2 copy-start.2
  86.1 142.9 %all-reduce.8.cloned.1.call-start = ((), (), s32[]{:S(2)}) async-start(), calls=%async_computation.2 | async-start | bytes 4194304 | tf_op jit(solution)/shard_map/psum | solution.py:32
  229.0 2.2 copy-start.1
Sparse Core Ops, SparseCore 0:
  18.5 54.0 all-reduce.3
  86.2 78.2 all-reduce.5
  178.0 50.9 all-reduce.7
where the time goes:
time: 240 us
  waiting for transfers between devices  182 us (76%)
  matrix products  31.8 us (13%)
  between operations  13.8 us (6%)
  other arithmetic  7.02 us (3%)
  local copies, waits for them, and re-layouts  4.7 us (2%)
    psum x1, waiting for transfers between devices, local(): cosample = scale_rows(lax.psum(backward(snapshots, sample), 'space'))  78.2 us
    psum x1, waiting for transfers between devices, local(): sample = scale_rows(lax.psum(forward(snapshots, sketch), 'tm'))  54.2 us
    psum x1, waiting for transfers between devices, local(): refined = scale_rows(lax.psum(forward(snapshots, cosample), 'tm'))  49.8 us
    dot_general x2, matrix products, forward(): jnp.dot(block, right, precision=lax.Precision.HIGHEST, preferred_element_...  20.6 us
    dot_general x1, matrix products, backward(): lax.dot_general(block, right, (((0,), (0,)), ((), ())), precision=lax.Pre...  11.2 us
    reduce_sum x3, other arithmetic, scale_rows(): jnp.mean(value * value, axis=1, keepdims=True) + EPS  5.33 us
  transfers between devices with their start and end apart: 3, of which 3 were waited for; matrix products, arithmetic and copies ran while one was open for 1% of the time, Pallas kernels for 0%

commit v1 on v0

--- a/solution.py
+++ b/solution.py
@@ -28,7 +28,7 @@
 
 def local(snapshots, sketch):
     sample = scale_rows(lax.psum(forward(snapshots, sketch), "tm"))
-    cosample = scale_rows(lax.psum(backward(snapshots, sample), "space"))
+    cosample = scale_rows(jnp.sum(lax.all_gather(backward(snapshots, sample), "space"), axis=0))
     refined = scale_rows(lax.psum(forward(snapshots, cosample), "tm"))
     return (refined, cosample)
 

time: 240 us -> 294 us (1.23)
  waiting for transfers between devices: 182 us -> 227 us
  local copies, waits for them, and re-layouts: 4.7 us -> 15.9 us
    all_gather x0 -> x1, waiting for transfers between devices: none -> 124 us  [local(): lax.all_gather(backward(snapshots, sample), 'space')]
    psum x1 -> x0, waiting for transfers between devices: 78.2 us -> none  [local(): cosample = scale_rows(lax.psum(backward(snapshots, sample), 'space'))]
    unnamed x8 -> x13, local copies, waits for them, and re-layouts: 4.7 us -> 15.9 us
  transfers between devices with their start and end apart: 3 -> 3, of which waited for: 3 -> 3; matrix products, arithmetic and copies ran while one was open for 1% -> 0% of each run, Pallas kernels for 0% -> 0%
where the time goes in v1:
time: 294 us
  waiting for transfers between devices  227 us (77%)
  matrix products  30 us (10%)
  local copies, waits for them, and re-layouts  15.9 us (5%)
  between operations  13.8 us (5%)
  other arithmetic  6.6 us (2%)
    all_gather x1, waiting for transfers between devices, local(): lax.all_gather(backward(snapshots, sample), 'space')  124 us
    psum x1, waiting for transfers between devices, local(): sample = scale_rows(lax.psum(forward(snapshots, sketch), 'tm'))  54.2 us
    psum x1, waiting for transfers between devices, local(): refined = scale_rows(lax.psum(forward(snapshots, cosample), 'tm'))  48.4 us
    dot_general x2, matrix products, forward(): jnp.dot(block, right, precision=lax.Precision.HIGHEST, preferred_element_...  18.8 us
    unnamed x13, local copies, waits for them, and re-layouts  15.9 us
    dot_general x1, matrix products, backward(): lax.dot_general(block, right, (((0,), (0,)), ((), ())), precision=lax.Pre...  11.2 us
  transfers between devices with their start and end apart: 3, of which 3 were waited for; matrix products, arithmetic and copies ran while one was open for 0% of the time, Pallas kernels for 0%

profile of v1, /device:TPU:0, one launch (start us, length us, event | category | flops | bytes accessed | tf_op | source)
XLA Modules:
  0.0 293.7 jit_solution(18023194598795867)
XLA Ops:
  7.2 0.0 all-reduce.3.cloned.1.call-start
  7.2 1.2 copy-done
  8.4 10.0 %fusion.6 = f32[2048,256]{1,0:T(8,128)} fusion(f32[2048,1024]{1,0:T(8,128)} %param.2, f32[1024,256]{1,0:T(8,128)S(1)} %copy-done), kind=kOutput, calls=%fused_computation.14 | convolution fusion | flops 6442450944 | bytes 11534336 | tf_op jit(solution)/shard_map/dot_general | solution.py:14
  18.4 0.0 all-reduce.3.cloned.1.call-update
  18.4 0.0 all-gather.3.cloned.1.call-start
  18.5 54.2 %all-reduce.3.cloned.1.call-done = f32[2048,256]{1,0:T(8,128)} async-done(((f32[2048,256]{1,0:T(8,128)}), f32[2048,256]{1,0:T(8,128)}) %all-reduce.3.cloned.1.call-update) | async-done | bytes 2097168 | tf_op jit(solution)/shard_map/psum | solution.py:30
  72.7 2.1 multiply_reduce_fusion.1
  74.8 0.1 copy-done.2
  74.9 11.2 %fusion.2 = f32[1024,256]{0,1:T(8,128)} fusion(f32[2048,1024]{1,0:T(8,128)} %param.2, f32[2048,256]{1,0:T(8,128)S(1)} %copy-done.2, f32[2048]{0:T(1024)S(1)} %add_rsqrt_fusion.1), kind=kOutput, calls=%fused_computation.6 | convolution fusion | flops 6442975232 | bytes 11542528 | tf_op jit(solution)/shard_map/dot_general | solution.py:20
  86.1 0.0 all-gather.3.cloned.1.call-update
  86.1 0.2 all-reduce.5.cloned.1.call-start
  86.3 124.4 %all-gather.3.cloned.1.call-done = f32[8192,256]{0,1:T(8,128)} async-done(((f32[1024,256]{0,1:T(8,128)}), f32[8192,256]{0,1:T(8,128)}) %all-gather.3.cloned.1.call-update) | async-done | bytes 8388624 | tf_op jit(solution)/shard_map/all_gather | solution.py:31
  210.8 11.2 %copy.7 = f32[32,8,8,1024]{3,2,1,0:T(8,128)S(1)} copy(f32[32,8,8,1024]{3,1,2,0:T(8,128)} %bitcast.16) | data formatting | bytes 16777216
  222.0 2.0 bitcast_reduce_fusion
  224.0 0.1 multiply_reduce_fusion.2
  224.1 0.2 broadcast_multiply_fusion.1
  224.3 8.8 %convolution_bitcast_fusion = f32[2048,256]{0,1:T(8,128)} fusion(f32[1024,256]{0,1:T(8,128)S(1)} %broadcast_multiply_fusion.1, f32[2048,1024]{1,0:T(8,128)S(1)} %bitcast.15), kind=kOutput, calls=%fused_computation.1 | convolution fusion | flops 6442450944 | bytes 11534336 | tf_op jit(solution)/shard_map/dot_general | solution.py:14
  233.1 0.0 all-reduce.5.cloned.1.call-update
  233.1 1.3 copy.6
  234.4 48.4 %all-reduce.5.cloned.1.call-done = f32[2048,256]{0,1:T(8,128)} async-done(((f32[2048,256]{0,1:T(8,128)}), f32[2048,256]{0,1:T(8,128)}) %all-reduce.5.cloned.1.call-update) | async-done | bytes 2097168 | tf_op jit(solution)/shard_map/psum | solution.py:32
  282.8 1.9 multiply_reduce_fusion
  284.8 0.3 copy-done.1
  285.0 0.3 broadcast_multiply_fusion
  285.4 1.8 copy.5
  (11 shorter events, 0.0 us)
Async XLA Ops:
  7.2 1.2 copy-start
  7.2 65.5 %all-reduce.3.cloned.1.call-start = ((), (), s32[]{:S(2)}) async-start(), calls=%async_computation | async-start | bytes 4194304 | tf_op jit(solution)/shard_map/psum | solution.py:30
  18.4 192.4 %all-gather.3.cloned.1.call-start = ((), (), s32[]{:S(2)}) async-start(), calls=%async_computation.2 | async-start | bytes 9437184 | tf_op jit(solution)/shard_map/all_gather | solution.py:31
  72.7 2.2 copy-start.2
  86.1 196.7 %all-reduce.5.cloned.1.call-start = ((), (), s32[]{:S(2)}) async-start(), calls=%async_computation.1 | async-start | bytes 4194304 | tf_op jit(solution)/shard_map/psum | solution.py:32
  210.8 13.5 %slice-start = ((s8[8388608]{0:T(1024)(128)(4,1)}), s8[4194304]{0:T(1024)(128)(4,1)S(1)}, s32[]{:S(2)}) async-start(s8[8388608]{0:T(1024)(128)(4,1)} %bitcast.14), calls=%async_computation.3 | async-start | bytes 8388608
  210.8 13.5 %slice-start.1 = ((s8[8388608]{0:T(1024)(128)(4,1)}), s8[4194304]{0:T(1024)(128)(4,1)S(1)}, s32[]{:S(2)}) async-start(s8[8388608]{0:T(1024)(128)(4,1)} %bitcast.14), calls=%async_computation.4 | async-start | bytes 8388608
  282.8 2.2 copy-start.1
Sparse Core Ops, SparseCore 0:
  18.5 54.0 all-reduce.2
  86.2 124.5 all-gather.2
  233.2 49.5 all-reduce.4
